TPU v7x, 32 devices: a whole 2x2x4 slice. The times are simulated.
32 devices in a mesh: dom: 8 (over y, x, core), col: 4 (over z).
Axes of the slice: x: 2, y: 2, z: 4, core: 2. Of those that a mesh axis runs over, the one named last changes fastest.
Arguments:
- features: bfloat16 [65536, 1024], P('dom', 'col')
- weight: bfloat16 [1024, 1024], P(None, 'col'), may hold values from -0.1875 to 0.1875
- out_bias: bfloat16 [1024], P('col'), may hold values from -3 to 3
- local_index: int32 [8, 64, 4], P('dom'), may hold values from 0 to 63
- local_count: int32 [8, 64], P('dom'), may hold values from 1 to 4, as said below
- local_vals: bfloat16 [8, 64, 4, 128, 128], P('dom'), may hold values from -0.1875 to 0.1875
- halo_index: int32 [8, 64, 4], P('dom'), may hold values from 0 to 31
- halo_count: int32 [8, 64], P('dom'), may hold values from 0 to 4, as said below
- halo_vals: bfloat16 [8, 64, 4, 128, 128], P('dom'), may hold values from -0.1875 to 0.1875
- send_rows: int32 [8, 8, 512], P('dom'), may hold values from 0 to 8191
- send_count: int32 [8, 8], P('dom'), may hold values from 0 to 512, as said below
Outputs:
- normalized: bfloat16 [65536, 1024], P('dom', 'col')
- channel_stats: float32 [2, 1024], P(None, 'col')
Inputs may be any that keep to these rules, and one draw needn't show every extreme that they name: `local_index`: slots k >= local_count of a row tile are not used. `local_count`: every partition has a row tile with all 4 slots used. `halo_index`: slots k >= halo_count of a row tile are not used. `halo_count`: every partition has a row tile with all 4 slots used. `send_rows`: slots s >= send_count[q, p] are not used. send_count[p, p] is 0; every partition fills all 512 slots to some other partition.
All inputs are finite; a program needn't handle non-finite values.
Results may differ from a plain program's by a relative error of at most 0.0075.
Values may be sent and summed in bfloat16 or wider, within the bound.
A program may use at most 192 MiB of HBM per device.

v0:
```python
import jax
import jax.numpy as jnp
from jax import lax
from jax.sharding import PartitionSpec as P

TILE = 128
epsilon = 1e-06


def tile_sum(sources, tile_index, tile_count, tile_vals):
    gathered = sources[tile_index]
    keep_mask = jnp.arange(tile_vals.shape[1])[None, :] < tile_count[:, None]
    masked = jnp.where(keep_mask[:, :, None, None], tile_vals, jnp.zeros_like(tile_vals))
    return jnp.einsum("tkij,tkjc->tic", masked, gathered, preferred_element_type=jnp.float32)


def on_device(
    features,
    weight,
    out_bias,
    local_index,
    local_count,
    local_vals,
    halo_index,
    halo_count,
    halo_vals,
    send_rows,
    send_count,
):
    row_count, col_width = features.shape
    peer_count = lax.axis_size("dom")
    slot_total = send_rows.shape[2]
    chosen = features[send_rows[0]]
    keep_mask = jnp.arange(slot_total)[None, :] < send_count[0][:, None]
    outgoing = jnp.where(keep_mask[:, :, None], chosen, jnp.zeros_like(chosen))
    arrived = lax.all_to_all(outgoing, "dom", split_axis=0, concat_axis=0, tiled=True)
    halo_tiles = arrived.reshape(peer_count * slot_total // TILE, TILE, col_width)
    own_tiles = features.reshape(row_count // TILE, TILE, col_width)
    summed = tile_sum(own_tiles, local_index[0], local_count[0], local_vals[0])
    summed = summed + tile_sum(halo_tiles, halo_index[0], halo_count[0], halo_vals[0])
    spread = summed.reshape(row_count, col_width).astype(jnp.bfloat16)
    node_total = row_count * peer_count
    regrouped = lax.all_to_all(spread, "col", split_axis=0, concat_axis=1, tiled=True)
    full_weight, full_bias = (
        lax.all_gather(weight, "col", axis=1, tiled=True),
        lax.all_gather(out_bias.reshape(1, col_width), "col", axis=1, tiled=True),
    )
    mixed_rows = jnp.dot(regrouped, full_weight, preferred_element_type=jnp.float32) + full_bias[
        0
    ].astype(jnp.float32)
    active = jnp.maximum(mixed_rows, 0.0)
    row_power = jnp.mean(active * active, axis=1, keepdims=True)
    scaled = active * lax.rsqrt(row_power + epsilon)
    sum_whole, square_whole = lax.psum(
        (jnp.sum(scaled, axis=0), jnp.sum(scaled * scaled, axis=0)), ("dom", "col")
    )
    normalized = lax.all_to_all(
        scaled.astype(jnp.bfloat16), "col", split_axis=1, concat_axis=0, tiled=True
    )
    column_start = lax.axis_index("col") * col_width
    sum_total = lax.dynamic_slice_in_dim(sum_whole, column_start, col_width, 0)
    square_total = lax.dynamic_slice_in_dim(square_whole, column_start, col_width, 0)
    channel_mean = sum_total / node_total
    channel_var = square_total / node_total - channel_mean * channel_mean
    return (normalized, jnp.stack([channel_mean, channel_var]))


def solution(mesh):
    in_specs = (
        P("dom", "col"),
        P(None, "col"),
        P("col"),
        P("dom", None, None),
        P("dom", None),
        P("dom", None, None, None, None),
        P("dom", None, None),
        P("dom", None),
        P("dom", None, None, None, None),
        P("dom", None, None),
        P("dom", None),
    )
    out_specs = (P("dom", "col"), P(None, "col"))
    return jax.shard_map(
        on_device, mesh=mesh, in_specs=in_specs, out_specs=out_specs, check_vma=False
    )
```

profile of v0, /device:TPU:0, one launch (start us, length us, event | category | flops | bytes accessed | tf_op | source)
XLA Modules:
  0.0 374.6 jit_solution(2426596609186330712)
XLA Ops:
  7.2 0.7 fusion.10
  7.9 0.7 iota_compare_fusion.2
  8.6 15.7 %gather_fusion.1 = bf16[4096,256]{1,0:T(8,128)(2,1)S(1)} fusion(bf16[8192,256]{1,0:T(8,128)(2,1)} %param.11, s32[4096]{0:T(1024)S(1)} %broadcast_clamp_fusion), kind=kCustom, calls=%fused_computation.1 | custom fusion | bytes 4210688 | tf_op jit(solution)/shard_map/gather | solution.py:33
  24.4 0.0 copy-start
  24.4 0.0 copy-start.1
  24.4 1.7 broadcast_select_fusion
  26.1 5.2 %all-to-all-start = ((bf16[8,512,256]{2,1,0:T(8,128)(2,1)}), bf16[8,512,256]{2,1,0:T(8,128)(2,1)S(1)}, u32[]{:S(2)}, u32[]{:S(2)}) async-start(bf16[8,512,256]{2,1,0:T(8,128)(2,1)} %broadcast_select_fusion), calls=%async_computation | async-start | bytes 4194304 | tf_op jit(solution)/shard_map/all_to_all | solution.py:36
  31.3 0.0 copy-done
  31.3 0.1 copy.19
  31.4 0.1 reshape.208
  31.5 0.0 copy-done.1
  31.5 0.1 copy.18
  31.6 0.1 reshape.192
  31.7 0.0 copy-start.2
  31.7 0.0 copy-start.3
  31.7 12.0 %gather_fusion = bf16[256,128,256]{2,1,0:T(8,128)(2,1)} fusion(bf16[64,128,256]{2,1,0:T(8,128)(2,1)} %bitcast.52, s32[1024]{0:T(1024)S(1)} %pad_clamp_fusion.1), kind=kCustom, calls=%fused_computation | custom fusion | bytes 33555456 | tf_op jit(solution)/shard_map/gather | solution.py:11
  43.7 0.0 copy-done.2
  43.7 0.1 iota_compare_fusion
  43.8 0.0 copy-done.3
  43.8 0.1 iota_compare_fusion.1
  43.9 14.0 %all-to-all-done = bf16[8,512,256]{2,1,0:T(8,128)(2,1)S(1)} async-done(((bf16[8,512,256]{2,1,0:T(8,128)(2,1)}), bf16[8,512,256]{2,1,0:T(8,128)(2,1)S(1)}, u32[]{:S(2)}, u32[]{:S(2)}) %all-to-all-start) | async-done | bytes 2097184 | tf_op jit(solution)/shard_map/all_to_all | solution.py:36
  57.9 9.7 %gather_fusion.2 = bf16[256,128,256]{2,1,0:T(8,128)(2,1)} fusion(bf16[32,128,256]{2,1,0:T(8,128)(2,1)S(1)} %bitcast.53, s32[1024]{0:T(1024)S(1)} %pad_clamp_fusion), kind=kCustom, calls=%fused_computation.2 | custom fusion | bytes 33555456 | tf_op jit(solution)/shard_map/gather | solution.py:11
  67.6 13.8 %fusion.1 = f32[64,128,256,1]{2,1,3,0:T(8,128)} fusion(bf16[64,4,128,256]{3,2,1,0:T(8,128)(2,1)} %bitcast.54, bf16[1,64,4,128,128]{4,3,2,1,0:T(8,128)(2,1)} %param.19, pred[64,4]{1,0:T(8,128)(4,1)S(1)} %iota_compare_fusion), kind=kOutput, calls=%fused_computation.6 | convolution fusion | flops 2151677952 | bytes 33554688 | tf_op jit(solution)/shard_map/tkij,tkjc->tic/dot_general | solution.py:14
  81.4 14.0 %fusion = bf16[64,128,256]{2,1,0:T(8,128)(2,1)} fusion(f32[64,128,256,1]{2,1,3,0:T(8,128)} %fusion.1, bf16[64,4,128,256]{3,2,1,0:T(8,128)(2,1)} %bitcast.55, bf16[1,64,4,128,128]{4,3,2,1,0:T(8,128)(2,1)} %param.16, pred[64,4]{1,0:T(8,128)(4,1)S(1)} %iota_compare_fusion.1), kind=kOutput, calls=%fused_computation.4 | convolution fusion | flops 2155872256 | bytes 37748992 | tf_op jit(solution)/shard_map/tkij,tkjc->tic/dot_general | solution.py:14
  95.4 0.0 copy-start.4
  95.4 6.3 %copy.20 = bf16[4,2048,256]{1,2,0:T(8,128)(2,1)} copy(bf16[4,2048,256]{2,1,0:T(8,128)(2,1)} %bitcast.56) | data formatting | bytes 8388608 | tf_op jit(solution)/shard_map/convert_element_type | solution.py:41
  101.6 4.9 %all-to-all-start.1 = ((bf16[4,2048,256]{1,2,0:T(8,128)(2,1)}), bf16[4,2048,256]{1,2,0:T(8,128)(2,1)}, u32[]{:S(2)}, u32[]{:S(2)}) async-start(bf16[4,2048,256]{1,2,0:T(8,128)(2,1)} %copy.20), calls=%async_computation.1 | async-start | bytes 8388608 | tf_op jit(solution)/shard_map/all_to_all | solution.py:43
  106.5 0.0 all-gather.4.cloned.1.call-start
  106.5 0.7 all-gather.4.cloned.1.call-update
  107.2 0.0 copy-done.4
  107.3 103.9 %all-gather.1 = bf16[4,1,256]{2,1,0:T(2,128)(2,1)S(1)} all-gather(bf16[1,1,256]{2,1,0:T(2,128)(2,1)S(1)} %reshape.220), channel_id=2, replica_groups=mesh['dom'=8,'col'=4] {'col'}, dimensions={0}, use_global_device_ids=true | all-gather | bytes 2560 | tf_op jit(solution)/shard_map/all_gather | solution.py:46
  211.2 0.0 all-gather.4.cloned.1.call-done
  211.2 19.8 %all-to-all-done.1 = bf16[4,2048,256]{1,2,0:T(8,128)(2,1)} async-done(((bf16[4,2048,256]{1,2,0:T(8,128)(2,1)}), bf16[4,2048,256]{1,2,0:T(8,128)(2,1)}, u32[]{:S(2)}, u32[]{:S(2)}) %all-to-all-start.1) | async-done | bytes 4194336 | tf_op jit(solution)/shard_map/all_to_all | solution.py:43
  231.0 7.8 %multiply_reduce_fusion.1 = (f32[2048]{0:T(1024)S(1)}, f32[2048,1024]{0,1:T(8,128)S(1)}) fusion(f32[1024]{0:T(1024)S(1)} %bitcast.61, bf16[2048,1024]{0,1:T(8,128)(2,1)} %bitcast.19, bf16[1024,1024]{1,0:T(8,128)(2,1)} %all-gather.4.cloned.1.call-done), kind=kOutput, calls=%fused_computation.10 | convolution fusion | flops 4303353856 | bytes 14692352 | tf_op jit(solution)/shard_map/dot_general | solution.py:48
  238.8 3.5 fusion.6
  242.2 4.8 %all-to-all-start.2 = ((bf16[2048,4,256]{0,2,1:T(8,128)(2,1)}), bf16[2048,4,256]{0,2,1:T(8,128)(2,1)}, u32[]{:S(2)}, u32[]{:S(2)}) async-start(bf16[2048,4,256]{0,2,1:T(8,128)(2,1)} %bitcast.57), calls=%async_computation.2 | async-start | bytes 8388608 | tf_op jit(solution)/shard_map/all_to_all | solution.py:57
  247.1 113.8 %all-reduce = (f32[1024]{0:T(1024)S(1)}, f32[1024]{0:T(1024)S(1)}) all-reduce(f32[1024]{0:T(1024)S(1)} %get-tuple-element.3, f32[1024]{0:T(1024)S(1)} %get-tuple-element.2), channel_id=1, replica_groups=mesh['dom'=8,'col'=4] {'dom','col'}, use_global_device_ids=true, to_apply=%region_4.5 | all-reduce | flops 2048 | bytes 16384 | tf_op jit(solution)/shard_map/psum | solution.py:54
  360.9 0.1 dynamic-slice_multiply_fusion
  361.0 0.6 pad_maximum_fusion
  361.5 0.0 all-to-all-done.2
  361.6 6.2 %copy.21 = bf16[4,2048,256]{2,1,0:T(8,128)(2,1)} copy(bf16[4,2048,256]{1,2,0:T(8,128)(2,1)} %bitcast.22) | data formatting | bytes 8388608 | tf_op jit(solution)/shard_map/all_to_all | solution.py:57
  (9 shorter events, 0.1 us)
Async XLA Ops:
  24.4 6.9 %copy-start = (s32[1,64,4]{1,2,0:T(4,128)S(1)}, s32[1,64,4]{1,2,0:T(4,128)}, u32[]{:S(2)}) copy-start(s32[1,64,4]{1,2,0:T(4,128)} %param.17) | copy-start | bytes 3076
  24.4 7.1 %copy-start.1 = (s32[1,64,4]{1,2,0:T(4,128)S(1)}, s32[1,64,4]{1,2,0:T(4,128)}, u32[]{:S(2)}) copy-start(s32[1,64,4]{1,2,0:T(4,128)} %param.14) | copy-start | bytes 3076
  26.1 31.8 %all-to-all-start = ((bf16[8,512,256]{2,1,0:T(8,128)(2,1)}), bf16[8,512,256]{2,1,0:T(8,128)(2,1)S(1)}, u32[]{:S(2)}, u32[]{:S(2)}) async-start(bf16[8,512,256]{2,1,0:T(8,128)(2,1)} %broadcast_select_fusion), calls=%async_computation | async-start | bytes 4194304 | tf_op jit(solution)/shard_map/all_to_all | solution.py:36
  31.7 12.0 %copy-start.2 = (s32[1,64]{1,0:T(1,128)S(1)}, s32[1,64]{1,0:T(1,128)}, u32[]{:S(2)}) copy-start(s32[1,64]{1,0:T(1,128)} %param.18) | copy-start | bytes 772
  31.7 12.1 %copy-start.3 = (s32[1,64]{1,0:T(1,128)S(1)}, s32[1,64]{1,0:T(1,128)}, u32[]{:S(2)}) copy-start(s32[1,64]{1,0:T(1,128)} %param.15) | copy-start | bytes 772
  95.4 11.9 %copy-start.4 = (bf16[256]{0:T(256)(128)(2,1)S(1)}, bf16[256]{0:T(256)(128)(2,1)}, u32[]{:S(2)}) copy-start(bf16[256]{0:T(256)(128)(2,1)} %param.13) | copy-start | bytes 1540
  101.6 129.3 %all-to-all-start.1 = ((bf16[4,2048,256]{1,2,0:T(8,128)(2,1)}), bf16[4,2048,256]{1,2,0:T(8,128)(2,1)}, u32[]{:S(2)}, u32[]{:S(2)}) async-start(bf16[4,2048,256]{1,2,0:T(8,128)(2,1)} %copy.20), calls=%async_computation.1 | async-start | bytes 8388608 | tf_op jit(solution)/shard_map/all_to_all | solution.py:43
  106.5 104.7 %all-gather.4.cloned.1.call-start = ((), (), s32[]{:S(2)}) async-start(), calls=%async_computation.3 | async-start | bytes 2621440 | tf_op jit(solution)/shard_map/all_gather | solution.py:45
  242.2 119.3 %all-to-all-start.2 = ((bf16[2048,4,256]{0,2,1:T(8,128)(2,1)}), bf16[2048,4,256]{0,2,1:T(8,128)(2,1)}, u32[]{:S(2)}, u32[]{:S(2)}) async-start(bf16[2048,4,256]{0,2,1:T(8,128)(2,1)} %bitcast.57), calls=%async_computation.2 | async-start | bytes 8388608 | tf_op jit(solution)/shard_map/all_to_all | solution.py:57
Sparse Core Ops, SparseCore 0:
  108.9 94.7 all-gather.3
where the time goes:
time: 375 us
  blocking collectives  218 us (58%)
  local copies, waits for them, and re-layouts  50.3 us (13%)
  matrix products  35.5 us (9%)
  waiting for transfers between devices  34.5 us (9%)
  starting transfers between devices  14.9 us (4%)
  between operations  14.2 us (4%)
  other arithmetic  7.48 us (2%)
    psum x1, blocking collectives, on_device(): lax.psum((jnp.sum(scaled, axis=0), jnp.sum(scaled * scaled, axis=0)), ('d...  114 us
    all_gather x1, blocking collectives, on_device(): lax.all_gather(out_bias.reshape(1, col_width), 'col', axis=1, tiled=True)  104 us
    dot_general x2, matrix products, tile_sum(): jnp.einsum('tkij,tkjc->tic', masked, gathered, preferred_element_type=jnp...  27.7 us
    gather x2, local copies, waits for them, and re-layouts, tile_sum(): gathered = sources[tile_index]  21.7 us
    all_to_all x1, waiting for transfers between devices, on_device(): lax.all_to_all(spread, 'col', split_axis=0, concat_axis=1, tiled=True)  19.8 us
    gather x1, local copies, waits for them, and re-layouts, on_device(): chosen = features[send_rows[0]]  15.7 us
    all_to_all x1, waiting for transfers between devices, on_device(): lax.all_to_all(outgoing, 'dom', split_axis=0, concat_axis=0, tiled=True)  14 us
    dot_general x1, matrix products, on_device(): jnp.dot(regrouped, full_weight, preferred_element_type=jnp.float32)  7.76 us
  transfers between devices with their start and end apart: 4, of which 2 were waited for; matrix products, arithmetic and copies ran while one was open for 4% of the time, Pallas kernels for 0%

commit v1 on v0

--- a/solution.py
+++ b/solution.py
@@ -5,6 +5,17 @@
 
 TILE = 128
 epsilon = 1e-06
+
+
+def cut_along(array, dim, length):
+    before, after = (array.shape[:dim], array.shape[dim + 1 :])
+    return jnp.moveaxis(array.reshape(*before, length, -1, *after), dim, 0)
+
+
+def laid_out(blocks, dim):
+    shape = list(blocks.shape[1:])
+    shape[dim] *= blocks.shape[0]
+    return jnp.moveaxis(blocks, 0, dim).reshape(shape)
 
 
 def tile_sum(sources, tile_index, tile_count, tile_vals):
@@ -33,7 +44,16 @@
     chosen = features[send_rows[0]]
     keep_mask = jnp.arange(slot_total)[None, :] < send_count[0][:, None]
     outgoing = jnp.where(keep_mask[:, :, None], chosen, jnp.zeros_like(chosen))
-    arrived = lax.all_to_all(outgoing, "dom", split_axis=0, concat_axis=0, tiled=True)
+    devices, here = (lax.axis_size("dom"), lax.axis_index("dom"))
+    tiles = cut_along(outgoing, 0, devices)
+    finished = [tiles[here]]
+    for step in range(1, devices):
+        sent = tiles[(here + step) % devices]
+        finished.append(
+            lax.ppermute(sent, "dom", [(i, (i + step) % devices) for i in range(devices)])
+        )
+    tiles = jnp.stack(finished)[(here - jnp.arange(devices)) % devices]
+    arrived = laid_out(tiles, 0)
     halo_tiles = arrived.reshape(peer_count * slot_total // TILE, TILE, col_width)
     own_tiles = features.reshape(row_count // TILE, TILE, col_width)
     summed = tile_sum(own_tiles, local_index[0], local_count[0], local_vals[0])

time: 375 us -> 386 us (1.029)
  local copies, waits for them, and re-layouts: 50.3 us -> 59.2 us
  waiting for transfers between devices: 34.5 us -> 27.8 us
  starting transfers between devices: 14.9 us -> 19.7 us
    all_to_all x1 -> x0, waiting for transfers between devices: 14 us -> none  [on_device(): lax.all_to_all(outgoing, 'dom', split_axis=0, concat_axis=0, tiled=True)]
    ppermute x0 -> x7, starting transfers between devices: none -> 9.8 us  [on_device(): lax.ppermute(sent, 'dom', [(i, (i + step) % devices) for i in range(devic...]
    ppermute x0 -> x7, waiting for transfers between devices: none -> 7.25 us  [on_device(): lax.ppermute(sent, 'dom', [(i, (i + step) % devices) for i in range(devic...]
    all_to_all x1 -> x0, starting transfers between devices: 5.2 us -> none  [on_device(): lax.all_to_all(outgoing, 'dom', split_axis=0, concat_axis=0, tiled=True)]
  transfers between devices with their start and end apart: 4 -> 10, of which waited for: 2 -> 4; matrix products, arithmetic and copies ran while one was open for 4% -> 4% of each run, Pallas kernels for 0% -> 0%
where the time goes in v1:
time: 386 us; the launch traced here: 385 us
  blocking collectives  221 us (57%)
  local copies, waits for them, and re-layouts  59.2 us (15%)
  matrix products  35.5 us (9%)
  waiting for transfers between devices  27.8 us (7%)
  starting transfers between devices  19.7 us (5%)
  between operations  14.3 us (4%)
  other arithmetic  7.8 us (2%)
    psum x1, blocking collectives, on_device(): lax.psum((jnp.sum(scaled, axis=0), jnp.sum(scaled * scaled, axis=0)), ('d...  113 us
    all_gather x1, blocking collectives, on_device(): lax.all_gather(out_bias.reshape(1, col_width), 'col', axis=1, tiled=True)  108 us
    dot_general x2, matrix products, tile_sum(): jnp.einsum('tkij,tkjc->tic', masked, gathered, preferred_element_type=jnp...  27.7 us
    gather x2, local copies, waits for them, and re-layouts, tile_sum(): gathered = sources[tile_index]  21.9 us
    all_to_all x1, waiting for transfers between devices, on_device(): lax.all_to_all(spread, 'col', split_axis=0, concat_axis=1, tiled=True)  19.8 us
    gather x1, local copies, waits for them, and re-layouts, on_device(): chosen = features[send_rows[0]]  18.7 us
    ppermute x7, starting transfers between devices, on_device(): lax.ppermute(sent, 'dom', [(i, (i + step) % devices) for i in range(devic...  9.8 us
    dot_general x1, matrix products, on_device(): jnp.dot(regrouped, full_weight, preferred_element_type=jnp.float32)  7.76 us
  transfers between devices with their start and end apart: 10, of which 4 were waited for; matrix products, arithmetic and copies ran while one was open for 4% of the time, Pallas kernels for 0%

profile of v1, /device:TPU:0, one launch (start us, length us, event | category | flops | bytes accessed | tf_op | source)
XLA Modules:
  0.0 384.9 jit_solution(8078427719252142260)
XLA Ops:
  7.3 0.7 fusion.10
  8.0 0.7 iota_compare_fusion.2
  8.7 18.7 %gather_fusion.1 = bf16[4096,256]{1,0:T(8,128)(2,1)} fusion(bf16[8192,256]{1,0:T(8,128)(2,1)} %param.11, s32[4096]{0:T(1024)S(1)} %broadcast_clamp_fusion), kind=kCustom, calls=%fused_computation.1 | custom fusion | bytes 4210688 | tf_op jit(solution)/shard_map/gather | solution.py:44
  27.4 2.0 broadcast_select_fusion
  29.4 1.3 constant_dynamic-slice_fusion
  30.7 0.5 collective-permute-start
  31.2 2.5 collective-permute-start.1
  33.7 2.4 collective-permute-start.2
  36.1 0.5 collective-permute-start.3
  36.6 0.1 collective-permute-start.4
  36.7 0.0 copy-done.2
  36.7 0.1 copy.18
  36.8 0.1 reshape.253
  36.9 0.1 copy.19
  37.0 0.1 reshape.279
  37.1 0.1 iota_compare_fusion
  37.2 0.1 iota_compare_fusion.1
  37.3 0.7 bitcast_dynamic-update-slice_fusion.7
  38.0 12.1 %gather_fusion = bf16[256,128,256]{2,1,0:T(8,128)(2,1)} fusion(bf16[64,128,256]{2,1,0:T(8,128)(2,1)} %bitcast.71, s32[1024]{0:T(1024)S(1)} %get-tuple-element.19), kind=kCustom, calls=%fused_computation | custom fusion | bytes 33555456 | tf_op jit(solution)/shard_map/gather | solution.py:22
  50.1 0.0 collective-permute-done
  50.1 1.4 collective-permute-start.5
  51.6 0.0 collective-permute-done.1
  51.6 2.4 collective-permute-start.6
  54.0 0.0 collective-permute-done.2
  54.1 0.0 collective-permute-done.3
  54.1 3.8 collective-permute-done.4
  57.9 1.3 collective-permute-done.5
  59.2 2.2 collective-permute-done.6
  61.4 0.0 copy-start.1
  61.4 1.3 copy-done.1
  62.7 2.3 gather_fusion.2
  65.0 9.7 %gather_fusion.3 = bf16[256,128,256]{2,1,0:T(8,128)(2,1)} fusion(bf16[32,128,256]{2,1,0:T(8,128)(2,1)S(1)} %bitcast.72, s32[1024]{0:T(1024)S(1)} %get-tuple-element.18), kind=kCustom, calls=%fused_computation.3 | custom fusion | bytes 33555456 | tf_op jit(solution)/shard_map/gather | solution.py:22
  74.8 13.8 %fusion.1 = f32[64,128,256,1]{2,1,3,0:T(8,128)} fusion(bf16[64,4,128,256]{3,2,1,0:T(8,128)(2,1)} %bitcast.73, bf16[1,64,4,128,128]{4,3,2,1,0:T(8,128)(2,1)} %param.19, pred[64,4]{1,0:T(8,128)(4,1)S(1)} %iota_compare_fusion), kind=kOutput, calls=%fused_computation.7 | convolution fusion | flops 2151677952 | bytes 33554688 | tf_op jit(solution)/shard_map/tkij,tkjc->tic/dot_general | solution.py:25
  88.5 14.0 %fusion = bf16[64,128,256]{2,1,0:T(8,128)(2,1)} fusion(f32[64,128,256,1]{2,1,3,0:T(8,128)} %fusion.1, bf16[64,4,128,256]{3,2,1,0:T(8,128)(2,1)} %bitcast.74, bf16[1,64,4,128,128]{4,3,2,1,0:T(8,128)(2,1)} %param.16, pred[64,4]{1,0:T(8,128)(4,1)S(1)} %iota_compare_fusion.1), kind=kOutput, calls=%fused_computation.5 | convolution fusion | flops 2155872256 | bytes 37748992 | tf_op jit(solution)/shard_map/tkij,tkjc->tic/dot_general | solution.py:25
  102.5 6.3 %copy.20 = bf16[4,2048,256]{1,2,0:T(8,128)(2,1)} copy(bf16[4,2048,256]{2,1,0:T(8,128)(2,1)} %bitcast.75) | data formatting | bytes 8388608 | tf_op jit(solution)/shard_map/convert_element_type | solution.py:61
  108.8 5.0 %all-to-all-start = ((bf16[4,2048,256]{1,2,0:T(8,128)(2,1)}), bf16[4,2048,256]{1,2,0:T(8,128)(2,1)}, u32[]{:S(2)}, u32[]{:S(2)}) async-start(bf16[4,2048,256]{1,2,0:T(8,128)(2,1)} %copy.20), calls=%async_computation | async-start | bytes 8388608 | tf_op jit(solution)/shard_map/all_to_all | solution.py:63
  113.8 0.0 all-gather.4.cloned.1.call-start
  113.9 0.7 all-gather.4.cloned.1.call-update
  114.6 107.6 %all-gather.1 = bf16[4,1,256]{2,1,0:T(2,128)(2,1)S(1)} all-gather(bf16[1,1,256]{2,1,0:T(2,128)(2,1)S(1)} %reshape.292), channel_id=2, replica_groups=mesh['dom'=8,'col'=4] {'col'}, dimensions={0}, use_global_device_ids=true | all-gather | bytes 2560 | tf_op jit(solution)/shard_map/all_gather | solution.py:66
  222.1 19.8 %all-to-all-done = bf16[4,2048,256]{1,2,0:T(8,128)(2,1)} async-done(((bf16[4,2048,256]{1,2,0:T(8,128)(2,1)}), bf16[4,2048,256]{1,2,0:T(8,128)(2,1)}, u32[]{:S(2)}, u32[]{:S(2)}) %all-to-all-start) | async-done | bytes 4194336 | tf_op jit(solution)/shard_map/all_to_all | solution.py:63
  242.0 7.8 %multiply_reduce_fusion.1 = (f32[2048]{0:T(1024)S(1)}, f32[2048,1024]{0,1:T(8,128)S(1)}) fusion(f32[1024]{0:T(1024)S(1)} %bitcast.81, bf16[2048,1024]{0,1:T(8,128)(2,1)} %bitcast.29, bf16[1024,1024]{1,0:T(8,128)(2,1)} %all-gather.4.cloned.1.call-done), kind=kOutput, calls=%fused_computation.11 | convolution fusion | flops 4303353856 | bytes 14692352 | tf_op jit(solution)/shard_map/dot_general | solution.py:68
  249.8 3.5 fusion.6
  253.2 4.8 %all-to-all-start.1 = ((bf16[2048,4,256]{0,2,1:T(8,128)(2,1)}), bf16[2048,4,256]{0,2,1:T(8,128)(2,1)}, u32[]{:S(2)}, u32[]{:S(2)}) async-start(bf16[2048,4,256]{0,2,1:T(8,128)(2,1)} %bitcast.76), calls=%async_computation.1 | async-start | bytes 8388608 | tf_op jit(solution)/shard_map/all_to_all | solution.py:77
  258.1 113.0 %all-reduce = (f32[1024]{0:T(1024)S(1)}, f32[1024]{0:T(1024)S(1)}) all-reduce(f32[1024]{0:T(1024)S(1)} %get-tuple-element.3, f32[1024]{0:T(1024)S(1)} %get-tuple-element.2), channel_id=1, replica_groups=mesh['dom'=8,'col'=4] {'dom','col'}, use_global_device_ids=true, to_apply=%region_4.5 | all-reduce | flops 2048 | bytes 16384 | tf_op jit(solution)/shard_map/psum | solution.py:74
  371.2 0.1 dynamic-slice_multiply_fusion
  371.2 0.6 pad_maximum_fusion
  371.8 0.0 all-to-all-done.1
  371.8 6.2 %copy.21 = bf16[4,2048,256]{2,1,0:T(8,128)(2,1)} copy(bf16[4,2048,256]{1,2,0:T(8,128)(2,1)} %bitcast.32) | data formatting | bytes 8388608 | tf_op jit(solution)/shard_map/all_to_all | solution.py:77
  (29 shorter events, 0.2 us)
Async XLA Ops:
  27.4 9.3 %copy-start.2 = (s32[1,64,4]{1,2,0:T(4,128)S(1)}, s32[1,64,4]{1,2,0:T(4,128)}, u32[]{:S(2)}) copy-start(s32[1,64,4]{1,2,0:T(4,128)} %param.14) | copy-start | bytes 3076
  27.4 9.5 %copy-start.3 = (s32[1,64,4]{1,2,0:T(4,128)S(1)}, s32[1,64,4]{1,2,0:T(4,128)}, u32[]{:S(2)}) copy-start(s32[1,64,4]{1,2,0:T(4,128)} %param.17) | copy-start | bytes 3076
  27.4 9.7 %copy-start.4 = (s32[1,64]{1,0:T(1,128)S(1)}, s32[1,64]{1,0:T(1,128)}, u32[]{:S(2)}) copy-start(s32[1,64]{1,0:T(1,128)} %param.18) | copy-start | bytes 772
  27.4 9.8 %copy-start.5 = (s32[1,64]{1,0:T(1,128)S(1)}, s32[1,64]{1,0:T(1,128)}, u32[]{:S(2)}) copy-start(s32[1,64]{1,0:T(1,128)} %param.15) | copy-start | bytes 772
  30.7 19.4 %collective-permute-start = (bf16[1,512,256]{2,1,0:T(8,128)(2,1)}, bf16[1,512,256]{2,1,0:T(8,128)(2,1)S(1)}, u32[]{:S(2)}, u32[]{:S(2)}) collective-permute-start(bf16[1,512,256]{2,1,0:T(8,128)(2,1)} %get-tuple-element.13), channel_id=1, source_target_pairs={{0,4},{4,8},{8,12},{12,16},{16,20},{20,24},{24,28},{28,0},{1,5},{5... | collective-permute-start | bytes 786440 | tf_op jit(solution)/shard_map/ppermute | solution.py:53
  31.2 20.4 %collective-permute-start.1 = (bf16[1,512,256]{2,1,0:T(8,128)(2,1)}, bf16[1,512,256]{2,1,0:T(8,128)(2,1)S(1)}, u32[]{:S(2)}, u32[]{:S(2)}) collective-permute-start(bf16[1,512,256]{2,1,0:T(8,128)(2,1)} %get-tuple-element.12), channel_id=1, source_target_pairs={{0,8},{4,12},{8,16},{12,20},{16,24},{20,28},{24,0},{28,4},{1,9},{5... | collective-permute-start | bytes 786440 | tf_op jit(solution)/shard_map/ppermute | solution.py:53
  33.7 20.4 %collective-permute-start.2 = (bf16[1,512,256]{2,1,0:T(8,128)(2,1)}, bf16[1,512,256]{2,1,0:T(8,128)(2,1)S(1)}, u32[]{:S(2)}, u32[]{:S(2)}) collective-permute-start(bf16[1,512,256]{2,1,0:T(8,128)(2,1)} %get-tuple-element.11), channel_id=1, source_target_pairs={{0,12},{4,16},{8,20},{12,24},{16,28},{20,0},{24,4},{28,8},{1,13},{... | collective-permute-start | bytes 786440 | tf_op jit(solution)/shard_map/ppermute | solution.py:53
  36.1 18.0 %collective-permute-start.3 = (bf16[1,512,256]{2,1,0:T(8,128)(2,1)}, bf16[1,512,256]{2,1,0:T(8,128)(2,1)S(1)}, u32[]{:S(2)}, u32[]{:S(2)}) collective-permute-start(bf16[1,512,256]{2,1,0:T(8,128)(2,1)} %get-tuple-element.10), channel_id=1, source_target_pairs={{0,16},{4,20},{8,24},{12,28},{16,0},{20,4},{24,8},{28,12},{1,17},{... | collective-permute-start | bytes 786440 | tf_op jit(solution)/shard_map/ppermute | solution.py:53
  36.6 21.3 %collective-permute-start.4 = (bf16[1,512,256]{2,1,0:T(8,128)(2,1)}, bf16[1,512,256]{2,1,0:T(8,128)(2,1)S(1)}, u32[]{:S(2)}, u32[]{:S(2)}) collective-permute-start(bf16[1,512,256]{2,1,0:T(8,128)(2,1)} %get-tuple-element.9), channel_id=1, source_target_pairs={{0,20},{4,24},{8,28},{12,0},{16,4},{20,8},{24,12},{28,16},{1,21},{... | collective-permute-start | bytes 786440 | tf_op jit(solution)/shard_map/ppermute | solution.py:53
  38.0 13.6 %copy-start = (bf16[8,1,512,256]{3,2,1,0:T(8,128)(2,1)S(1)}, bf16[8,1,512,256]{3,2,1,0:T(8,128)(2,1)}, u32[]{:S(2)}) copy-start(bf16[8,1,512,256]{3,2,1,0:T(8,128)(2,1)} %bitcast_dynamic-update-slice_fusion.7) | copy-start | bytes 6291460
  50.1 9.1 %collective-permute-start.5 = (bf16[1,512,256]{2,1,0:T(8,128)(2,1)}, bf16[1,512,256]{2,1,0:T(8,128)(2,1)S(1)}, u32[]{:S(2)}, u32[]{:S(2)}) collective-permute-start(bf16[1,512,256]{2,1,0:T(8,128)(2,1)} %get-tuple-element.8), channel_id=1, source_target_pairs={{0,24},{4,28},{8,0},{12,4},{16,8},{20,12},{24,16},{28,20},{1,25},{... | collective-permute-start | bytes 786440 | tf_op jit(solution)/shard_map/ppermute | solution.py:53
  51.6 9.8 %collective-permute-start.6 = (bf16[1,512,256]{2,1,0:T(8,128)(2,1)}, bf16[1,512,256]{2,1,0:T(8,128)(2,1)S(1)}, u32[]{:S(2)}, u32[]{:S(2)}) collective-permute-start(bf16[1,512,256]{2,1,0:T(8,128)(2,1)} %get-tuple-element.7), channel_id=1, source_target_pairs={{0,28},{4,0},{8,4},{12,8},{16,12},{20,16},{24,20},{28,24},{1,29},{... | collective-permute-start | bytes 786440 | tf_op jit(solution)/shard_map/ppermute | solution.py:53
  61.4 1.3 copy-start.1
  108.8 5.7 %copy-start.6 = (bf16[256]{0:T(256)(128)(2,1)S(1)}, bf16[256]{0:T(256)(128)(2,1)}, u32[]{:S(2)}) copy-start(bf16[256]{0:T(256)(128)(2,1)} %param.13) | copy-start | bytes 1540
  108.8 133.1 %all-to-all-start = ((bf16[4,2048,256]{1,2,0:T(8,128)(2,1)}), bf16[4,2048,256]{1,2,0:T(8,128)(2,1)}, u32[]{:S(2)}, u32[]{:S(2)}) async-start(bf16[4,2048,256]{1,2,0:T(8,128)(2,1)} %copy.20), calls=%async_computation | async-start | bytes 8388608 | tf_op jit(solution)/shard_map/all_to_all | solution.py:63
  113.8 108.3 %all-gather.4.cloned.1.call-start = ((), (), s32[]{:S(2)}) async-start(), calls=%async_computation.2 | async-start | bytes 2621440 | tf_op jit(solution)/shard_map/all_gather | solution.py:65
  253.2 118.6 %all-to-all-start.1 = ((bf16[2048,4,256]{0,2,1:T(8,128)(2,1)}), bf16[2048,4,256]{0,2,1:T(8,128)(2,1)}, u32[]{:S(2)}, u32[]{:S(2)}) async-start(bf16[2048,4,256]{0,2,1:T(8,128)(2,1)} %bitcast.76), calls=%async_computation.1 | async-start | bytes 8388608 | tf_op jit(solution)/shard_map/all_to_all | solution.py:77
Sparse Core Ops, SparseCore 0:
  116.2 99.3 all-gather.3
